TPU v7x, 32 devices: a whole 2x2x4 slice. The times are simulated.
32 devices in a mesh: member: 4 (over y, x), space: 8 (over z, core).
Axes of the slice: x: 2, y: 2, z: 4, core: 2. Of those that a mesh axis runs over, the one named last changes fastest.
Arguments:
- hidden_codes: bfloat16 [8, 256, 23040], P('member', None, 'space'), may hold values from -6 to 6
- w_in: bfloat16 [1024, 256], replicated, may hold values from -0.375 to 0.375
- b_in: float32 [1024], replicated, may hold values from -3 to 3
- w_out: bfloat16 [72, 1024], replicated, may hold values from -0.1875 to 0.1875
- b_out: float32 [72], replicated, may hold values from -3 to 3
- target: bfloat16 [72, 23040], P(None, 'space'), may hold values from -6 to 6
- band_start: int32 [8], P('space'), may hold values from 0 to 14, as said below
Outputs:
- code_sensitivity: bfloat16 [8, 256, 23040], P('member', None, 'space')
- grad_w_in: float32 [1024, 256], replicated
- grad_w_out: float32 [72, 1024], replicated
- grad_b_in: float32 [1024], replicated
Inputs may be any that keep to these rules, and one draw needn't show every extreme that they name: band_start holds each of 0, 2, 4, ... once, in some order.
All inputs are finite; a program needn't handle non-finite values.
Results may differ from a plain program's by a relative error of at most 0.005.
The roundings to bfloat16 on the way count: a program that leaves them out, or rounds other values in their place, can miss the bound.
Values may be sent and summed in bfloat16 or wider, within the bound.
A program may use at most 128 MiB of HBM per device.

v0:
```python
import math

import jax
import jax.numpy as jnp
from jax import lax
from jax.sharding import PartitionSpec as P

LON = 1440


def slope(diff):
    return diff / jnp.sqrt(diff * diff + 0.0625)


def pairwise_total(values, tiles):

    def lone_realization(total, other):
        return (total + slope(values - other.astype(jnp.float32)[None]), None)

    total, discarded_value = lax.scan(lone_realization, jnp.zeros_like(values), tiles)
    return total


def on_device(hidden_codes, w_in, b_in, w_out, b_out, target, band_start):
    local_members = hidden_codes.shape[0]
    cells = hidden_codes.shape[2]
    rows = cells // LON
    lat_rows = rows * lax.axis_size("space")
    members = local_members * lax.axis_size("member")
    angle = ((band_start[0] + jnp.arange(rows, dtype=jnp.int32)).astype(jnp.float32) + 0.5) * (
        math.pi / lat_rows
    ) - math.pi / 2
    area = jnp.broadcast_to(jnp.cos(angle)[:, None], (rows, LON)).reshape(cells)
    saved = []
    mapped_predictions = []
    for ensemble_position in range(local_members):
        pre = (
            jnp.dot(w_in, hidden_codes[ensemble_position], preferred_element_type=jnp.float32)
            + b_in[:, None]
        )
        act_f, undo = jax.vjp(jax.nn.gelu, pre)
        act = act_f.astype(jnp.bfloat16)
        saved.append((act, undo))
        mapped_predictions.append(
            (jnp.dot(w_out, act, preferred_element_type=jnp.float32) + b_out[:, None]).astype(
                jnp.bfloat16
            )
        )
    predicted_maps = jnp.stack(mapped_predictions)
    diagonal_contribution = predicted_maps.astype(jnp.float32)
    couple_index = pairwise_total(
        diagonal_contribution, lax.all_gather(predicted_maps, "member", axis=0, tiled=True)
    )
    goal = target.astype(jnp.float32)[None]
    prediction_sensitivity = (
        area[None, None, :] * (slope(diagonal_contribution - goal) - couple_index / members)
    ).astype(jnp.bfloat16)
    adjoint_entry_matrix = jnp.zeros(w_in.shape, jnp.float32)
    adjoint_exit_matrix = jnp.zeros(w_out.shape, jnp.float32)
    g_bias = jnp.zeros(b_in.shape, jnp.float32)
    grads = []
    for ensemble_position in range(local_members):
        act, undo = saved[ensemble_position]
        prediction_adjoint = prediction_sensitivity[ensemble_position]
        dact = jnp.dot(w_out.T, prediction_adjoint, preferred_element_type=jnp.float32)
        dpre = undo(dact)[0].astype(jnp.bfloat16)
        grads.append(jnp.dot(w_in.T, dpre, preferred_element_type=jnp.float32).astype(jnp.bfloat16))
        adjoint_entry_matrix = adjoint_entry_matrix + jnp.dot(
            dpre, hidden_codes[ensemble_position].T, preferred_element_type=jnp.float32
        )
        adjoint_exit_matrix = adjoint_exit_matrix + jnp.dot(
            prediction_adjoint, act.T, preferred_element_type=jnp.float32
        )
        g_bias = g_bias + jnp.sum(dpre.astype(jnp.float32), axis=1)
    code_sensitivity = jnp.stack(grads)
    stacked = jnp.concatenate(
        [adjoint_entry_matrix, adjoint_exit_matrix.T, g_bias[:, None]], axis=1
    )
    shares = lax.psum_scatter(
        stacked.astype(jnp.bfloat16), "space", scatter_dimension=0, tiled=True
    ).astype(jnp.float32)
    shares = lax.psum(shares, "member")
    summed = lax.all_gather(shares, "space", axis=0, tiled=True)
    scale = 1.0 / math.sqrt(members * cells)
    latent_width = w_in.shape[1]
    channel_count = w_out.shape[0]
    grad_w_in = summed[:, :latent_width] * scale
    grad_w_out = summed[:, latent_width : latent_width + channel_count].T * scale
    grad_b_in = summed[:, latent_width + channel_count] * scale
    return (code_sensitivity, grad_w_in, grad_w_out, grad_b_in)


def solution(mesh):
    in_specs = (P("member", None, "space"), P(), P(), P(), P(), P(None, "space"), P("space"))
    out_specs = (P("member", None, "space"), P(), P(), P())
    return jax.shard_map(
        on_device, mesh=mesh, in_specs=in_specs, out_specs=out_specs, check_vma=False
    )
```

profile of v0, /device:TPU:0, one launch (start us, length us, event | category | flops | bytes accessed | tf_op | source)
XLA Modules:
  0.0 237.3 jit_solution(15902013132649243403)
XLA Ops:
  7.2 0.0 copy-start
  7.2 0.0 copy-start.4
  7.2 0.0 all-gather.3.cloned.1.call-start
  7.2 1.0 copy-done
  8.2 7.4 %fusion.28 = f32[1024,2880]{0,1:T(8,128)} fusion(bf16[1024,256]{1,0:T(8,128)(2,1)S(1)} %copy-done, bf16[2,256,2880]{1,2,0:T(8,128)(2,1)} %param.9), kind=kOutput, calls=%fused_computation.48 | convolution fusion | flops 1509949440 | bytes 13795328 | tf_op jit(solution)/shard_map/dot_general | solution.py:38
  15.6 12.6 %multiply_convert_fusion.1 = (bf16[1024,2880]{0,1:T(8,128)(2,1)S(1)}, bf16[1024,2880]{0,1:T(8,128)(2,1)S(1)}, f32[1024,2880]{0,1:T(8,128)}) fusion(f32[1024]{0:T(1024)S(1)} %copy-done.10, f32[1024,2880]{0,1:T(8,128)} %fusion.28, bf16[1024,256]{1,0:T(8,128)(2,1)S(1)} %copy-done, bf16[2,256,2880]{1,2,0:T(8,128)(2,1)S(1)} %copy-done.4), kind=kOutput, calls=%fused_computation.33 | convolution fusion | flops 1568931840 | bytes 37392384 | tf_op jit(solution)/shard_map/dot_general | solution.py:38
  28.3 1.9 fusion.24
  30.2 0.0 copy-start.8
  30.2 1.9 fusion.25
  32.2 0.3 copy-done.2
  32.5 1.1 fusion.47
  33.6 0.0 all-gather.3.cloned.1.call-update
  33.6 0.2 reduce-scatter.4.cloned.1.call-start
  33.9 1.0 convert_element_type.72
  35.5 0.1 broadcast_in_dim.4
  35.6 0.1 mul.128
  35.7 46.7 %all-gather.3.cloned.1.call-done = bf16[8,72,2880]{2,1,0:T(8,128)(2,1)} async-done(((bf16[2,72,2880]{2,1,0:T(8,128)(2,1)}), bf16[8,72,2880]{2,1,0:T(8,128)(2,1)}) %all-gather.3.cloned.1.call-update) | async-done | bytes 3317776 | tf_op jit(solution)/shard_map/all_gather | solution.py:52
  82.4 31.5 %while.11 = (s32[]{:T(128)}, f32[2,72,2880]{2,1,0:T(8,128)}, bf16[8,72,2880]{2,1,0:T(8,128)(2,1)}, f32[2,72,2880]{2,1,0:T(8,128)S(1)}, s32[]{:T(128)}, /*index=5*/s32[]{:T(128)}) while((s32[]{:T(128)}, f32[2,72,2880]{2,1,0:T(8,128)}, bf16[8,72,2880]{2,1,0:T(8,128)(2,1)}, f32[2,72,2880]{2,1,0:T(8,128)S(1)}, s32[]{:T(128)}, ...), condition=%wide.region_1.2_spmd.clone, body=%wide.region_0.1_spmd.clone.sunk | while | flops 2695683 | bytes 7050323 | solution.py:20
  82.4 1.1 bitcast_convert_fusion.2
  83.5 1.6 select_add_fusion.2
  85.1 1.1 bitcast_convert_fusion.2
  86.1 3.0 %select_add_fusion.2 = f32[2,72,2880]{2,1,0:T(8,128)} fusion(f32[2,72,2880]{2,1,0:T(8,128)} %get-tuple-element.99, f32[2,72,2880]{2,1,0:T(8,128)S(1)} %get-tuple-element.107, f32[72,2880]{1,0:T(8,128)S(1)} %bitcast_convert_fusion.2, pred[]{:T(512)S(6)} %compare.3), kind=kLoop, calls=%fused_computation.clone.1 | loop fusion | flops 2488320 | bytes 5806081 | tf_op jit(solution)/shard_map/while/body/eval_jaxpr/add | solution.py:18
  89.2 1.1 bitcast_convert_fusion.2
  90.3 3.0 %select_add_fusion.2 = f32[2,72,2880]{2,1,0:T(8,128)} fusion(f32[2,72,2880]{2,1,0:T(8,128)} %get-tuple-element.99, f32[2,72,2880]{2,1,0:T(8,128)S(1)} %get-tuple-element.107, f32[72,2880]{1,0:T(8,128)S(1)} %bitcast_convert_fusion.2, pred[]{:T(512)S(6)} %compare.3), kind=kLoop, calls=%fused_computation.clone.1 | loop fusion | flops 2488320 | bytes 5806081 | tf_op jit(solution)/shard_map/while/body/eval_jaxpr/add | solution.py:18
  93.3 1.1 bitcast_convert_fusion.2
  94.4 3.0 %select_add_fusion.2 = f32[2,72,2880]{2,1,0:T(8,128)} fusion(f32[2,72,2880]{2,1,0:T(8,128)} %get-tuple-element.99, f32[2,72,2880]{2,1,0:T(8,128)S(1)} %get-tuple-element.107, f32[72,2880]{1,0:T(8,128)S(1)} %bitcast_convert_fusion.2, pred[]{:T(512)S(6)} %compare.3), kind=kLoop, calls=%fused_computation.clone.1 | loop fusion | flops 2488320 | bytes 5806081 | tf_op jit(solution)/shard_map/while/body/eval_jaxpr/add | solution.py:18
  97.4 1.1 bitcast_convert_fusion.2
  98.5 3.0 %select_add_fusion.2 = f32[2,72,2880]{2,1,0:T(8,128)} fusion(f32[2,72,2880]{2,1,0:T(8,128)} %get-tuple-element.99, f32[2,72,2880]{2,1,0:T(8,128)S(1)} %get-tuple-element.107, f32[72,2880]{1,0:T(8,128)S(1)} %bitcast_convert_fusion.2, pred[]{:T(512)S(6)} %compare.3), kind=kLoop, calls=%fused_computation.clone.1 | loop fusion | flops 2488320 | bytes 5806081 | tf_op jit(solution)/shard_map/while/body/eval_jaxpr/add | solution.py:18
  101.5 1.1 bitcast_convert_fusion.2
  102.6 3.0 %select_add_fusion.2 = f32[2,72,2880]{2,1,0:T(8,128)} fusion(f32[2,72,2880]{2,1,0:T(8,128)} %get-tuple-element.99, f32[2,72,2880]{2,1,0:T(8,128)S(1)} %get-tuple-element.107, f32[72,2880]{1,0:T(8,128)S(1)} %bitcast_convert_fusion.2, pred[]{:T(512)S(6)} %compare.3), kind=kLoop, calls=%fused_computation.clone.1 | loop fusion | flops 2488320 | bytes 5806081 | tf_op jit(solution)/shard_map/while/body/eval_jaxpr/add | solution.py:18
  105.6 1.1 bitcast_convert_fusion.2
  106.7 3.0 %select_add_fusion.2 = f32[2,72,2880]{2,1,0:T(8,128)} fusion(f32[2,72,2880]{2,1,0:T(8,128)} %get-tuple-element.99, f32[2,72,2880]{2,1,0:T(8,128)S(1)} %get-tuple-element.107, f32[72,2880]{1,0:T(8,128)S(1)} %bitcast_convert_fusion.2, pred[]{:T(512)S(6)} %compare.3), kind=kLoop, calls=%fused_computation.clone.1 | loop fusion | flops 2488320 | bytes 5806081 | tf_op jit(solution)/shard_map/while/body/eval_jaxpr/add | solution.py:18
  109.8 1.1 bitcast_convert_fusion.2
  110.8 3.0 %select_add_fusion.2 = f32[2,72,2880]{2,1,0:T(8,128)} fusion(f32[2,72,2880]{2,1,0:T(8,128)} %get-tuple-element.99, f32[2,72,2880]{2,1,0:T(8,128)S(1)} %get-tuple-element.107, f32[72,2880]{1,0:T(8,128)S(1)} %bitcast_convert_fusion.2, pred[]{:T(512)S(6)} %compare.3), kind=kLoop, calls=%fused_computation.clone.1 | loop fusion | flops 2488320 | bytes 5806081 | tf_op jit(solution)/shard_map/while/body/eval_jaxpr/add | solution.py:18
  113.9 2.5 %multiply_convert_fusion.2 = bf16[2,72,2880]{2,1,0:T(8,128)(2,1)S(1)} fusion(f32[2,72,2880]{2,1,0:T(8,128)} %get-tuple-element.26, f32[72,2880]{1,0:T(8,128)} %convert_element_type.72, f32[2880]{0:T(1024)S(1)} %mul.128, bf16[1,72,2880]{2,1,0:T(8,128)(2,1)S(1)} %fusion.24, bf16[1,72,2880]{2,1,0:T(8,128)(2,1)} %copy-done.3), kind=kLoop, calls=%fused_computation.45 | loop fusion | flops 4976640 | bytes 4158720 | tf_op jit(solution)/shard_map/convert_element_type | solution.py:57
  116.4 0.0 slice-start.8
  116.4 12.9 %convert_reduce_fusion = (f32[1024]{0:T(1024)S(1)}, bf16[1024,2880]{0,1:T(8,128)(2,1)S(1)}) fusion(f32[1024,2880]{0,1:T(8,128)} %fusion.28, f32[1024]{0:T(1024)S(1)} %copy-done.10, bf16[72,1024]{1,0:T(8,128)(2,1)} %param.12, bf16[2,72,2880]{2,1,0:T(8,128)(2,1)S(1)} %multiply_convert_fusion.2), kind=kOutput, calls=%fused_computation.30 | convolution fusion | flops 492502016 | bytes 18274304 | tf_op jit(solution)/shard_map/dot_general | solution.py:65
  129.3 0.0 copy-start.7
  129.3 1.2 fusion.45
  130.5 0.0 copy-start.5
  130.6 9.3 %convert_reduce_fusion.1 = (f32[1024]{0:T(1024)S(1)}, bf16[1024,2880]{0,1:T(8,128)(2,1)S(1)}) fusion(f32[1024,2880]{0,1:T(8,128)S(1)} %bitcast.105, f32[1024]{0:T(1024)S(1)} %copy-done.10, bf16[72,1024]{1,0:T(8,128)(2,1)S(1)} %copy-done.7, bf16[2,72,2880]{2,1,0:T(8,128)(2,1)S(1)} %multiply_convert_fusion.2), kind=kOutput, calls=%fused_computation.31 | convolution fusion | flops 492502016 | bytes 18274304 | tf_op jit(solution)/shard_map/dot_general | solution.py:65
  139.9 0.0 slice-start
  139.9 1.8 fusion.26
  141.8 2.4 %slice-done = s8[4194304]{0:T(1024)(128)(4,1)S(1)} async-done(((s8[5898240]{0:T(1024)(128)(4,1)}), s8[4194304]{0:T(1024)(128)(4,1)S(1)}, s32[]{:S(2)}) %slice-start) | async-done | bytes 4194328
  144.2 0.5 slice-done.1
  144.7 1.2 fusion.44
  145.9 1.8 fusion.37
  147.8 0.1 pad_maximum_fusion.2
  147.8 1.2 copy.13
  149.0 0.0 reduce-scatter.4.cloned.1.call-update
  149.0 0.0 all-gather.5.cloned.1.call-start
  149.1 32.0 %reduce-scatter.4.cloned.1.call-done = bf16[128,329]{1,0:T(8,128)(2,1)} async-done(((bf16[1024,329]{1,0:T(8,128)(2,1)}), bf16[128,329]{1,0:T(8,128)(2,1)}) %reduce-scatter.4.cloned.1.call-update) | async-done | bytes 84240
  181.0 1.0 copy.14
  182.1 19.8 %all-reduce.1 = f32[128,329]{0,1:T(8,128)} all-reduce(bf16[128,329]{0,1:T(8,128)(2,1)S(1)} %copy.14), channel_id=1, replica_groups=mesh['member'=4,'space'=8] {'member'}, use_global_device_ids=true, to_apply=%region_5.6 | all-reduce | flops 42112 | bytes 252672 | tf_op jit(solution)/shard_map/psum | solution.py:82
  201.9 0.0 all-gather.5.cloned.1.call-update
  201.9 0.0 slice-start.5
  201.9 4.5 %fusion.20 = bf16[1,256,2880]{1,2,0:T(8,128)(2,1)S(1)} fusion(bf16[1024,2880]{0,1:T(8,128)(2,1)} %copy-done.11, bf16[1024,256]{1,0:T(8,128)(2,1)S(1)} %copy-done), kind=kOutput, calls=%fused_computation.36 | convolution fusion | flops 1510686720 | bytes 7897088 | tf_op jit(solution)/shard_map/dot_general | solution.py:67
  206.5 1.8 fusion.21
  208.2 1.9 pad_maximum_fusion
  210.1 14.9 %all-gather.5.cloned.1.call-done = f32[1024,329]{0,1:T(8,128)} async-done(((f32[128,329]{0,1:T(8,128)}), f32[1024,329]{0,1:T(8,128)}) %all-gather.5.cloned.1.call-update) | async-done | bytes 1347600 | tf_op jit(solution)/shard_map/all_gather | solution.py:83
  225.0 1.3 slice_multiply_fusion
  226.4 1.3 copy.12
  227.7 1.7 fusion.46
  229.4 1.4 slice_multiply_fusion.2
  (40 shorter events, 0.1 us)
Async XLA Ops:
  7.2 1.0 copy-start
  7.2 8.5 %copy-start.4 = (bf16[2,256,2880]{1,2,0:T(8,128)(2,1)S(1)}, bf16[2,256,2880]{1,2,0:T(8,128)(2,1)}, u32[]{:S(2)}) copy-start(bf16[2,256,2880]{1,2,0:T(8,128)(2,1)} %param.9) | copy-start | bytes 8847364
  7.2 8.4 %copy-start.10 = (f32[1024]{0:T(1024)S(1)}, f32[1024]{0:T(1024)}, u32[]{:S(2)}) copy-start(f32[1024]{0:T(1024)} %param.11) | copy-start | bytes 12292
  7.2 75.2 %all-gather.3.cloned.1.call-start = ((), (), s32[]{:S(2)}) async-start(), calls=%async_computation.1 | async-start | bytes 4239360 | tf_op jit(solution)/shard_map/all_gather | solution.py:52
  15.6 12.6 %copy-start.6 = (bf16[72,1024]{1,0:T(8,128)(2,1)S(1)}, bf16[72,1024]{1,0:T(8,128)(2,1)}, u32[]{:S(2)}) copy-start(bf16[72,1024]{1,0:T(8,128)(2,1)} %param.12) | copy-start | bytes 442372
  15.6 12.6 %copy-start.9 = (f32[72]{0:T(128)S(1)}, f32[72]{0:T(128)}, u32[]{:S(2)}) copy-start(f32[72]{0:T(128)} %param.13) | copy-start | bytes 868
  28.2 3.9 %copy-start.1 = (bf16[1024,2880]{0,1:T(8,128)(2,1)}, bf16[1024,2880]{0,1:T(8,128)(2,1)S(1)}, u32[]{:S(2)}) copy-start(bf16[1024,2880]{0,1:T(8,128)(2,1)S(1)} %get-tuple-element.61) | copy-start | bytes 17694724
  28.3 4.3 %copy-start.2 = (bf16[1024,2880]{0,1:T(8,128)(2,1)}, bf16[1024,2880]{0,1:T(8,128)(2,1)S(1)}, u32[]{:S(2)}) copy-start(bf16[1024,2880]{0,1:T(8,128)(2,1)S(1)} %get-tuple-element.60) | copy-start | bytes 17694724
  30.2 3.7 %copy-start.8 = (bf16[72,2880]{1,0:T(8,128)(2,1)S(1)}, bf16[72,2880]{1,0:T(8,128)(2,1)}, u32[]{:S(2)}) copy-start(bf16[72,2880]{1,0:T(8,128)(2,1)} %param.14) | copy-start | bytes 1244164
  32.5 1.1 copy-start.3
  33.6 147.4 %reduce-scatter.4.cloned.1.call-start = ((), (), s32[]{:S(2)}) async-start(), calls=%async_computation.3 | async-start | bytes 884736
  113.9 15.4 %slice-start.2 = ((s8[5898240]{0:T(1024)(128)(4,1)}), s8[4194304]{0:T(1024)(128)(4,1)S(1)}, s32[]{:S(2)}) async-start(s8[5898240]{0:T(1024)(128)(4,1)} %bitcast.99), calls=%async_computation.6 | async-start | bytes 8388608
  113.9 16.6 %slice-start.6 = ((s8[11796480]{0:T(1024)(128)(4,1)}), s8[4194304]{0:T(1024)(128)(4,1)S(1)}, s32[]{:S(2)}) async-start(s8[11796480]{0:T(1024)(128)(4,1)} %bitcast.104), calls=%async_computation.10 | async-start | bytes 8388608
  116.3 13.0 %slice-start.3 = ((s8[5898240]{0:T(1024)(128)(4,1)}), s8[1703936]{0:T(1024)(128)(4,1)S(1)}, s32[]{:S(2)}) async-start(s8[5898240]{0:T(1024)(128)(4,1)} %bitcast.99), calls=%async_computation.7 | async-start | bytes 3407872
  116.4 14.2 %slice-start.7 = ((s8[11796480]{0:T(1024)(128)(4,1)}), s8[4194304]{0:T(1024)(128)(4,1)S(1)}, s32[]{:S(2)}) async-start(s8[11796480]{0:T(1024)(128)(4,1)} %bitcast.104), calls=%async_computation.11 | async-start | bytes 8388608
  116.4 14.2 %slice-start.8 = ((s8[11796480]{0:T(1024)(128)(4,1)}), s8[3407872]{0:T(1024)(128)(4,1)S(1)}, s32[]{:S(2)}) async-start(s8[11796480]{0:T(1024)(128)(4,1)} %bitcast.104), calls=%async_computation.12 | async-start | bytes 6815744
  129.3 10.6 %copy-start.12 = (bf16[1024,2880]{0,1:T(8,128)(2,1)}, bf16[1024,2880]{0,1:T(8,128)(2,1)S(1)}, u32[]{:S(2)}) copy-start(bf16[1024,2880]{0,1:T(8,128)(2,1)S(1)} %get-tuple-element.66) | copy-start | bytes 17694724
  129.3 1.2 copy-start.7
  130.5 9.3 %copy-start.5 = (bf16[2,256,2880]{1,2,0:T(8,128)(2,1)S(1)}, bf16[2,256,2880]{1,2,0:T(8,128)(2,1)}, u32[]{:S(2)}) copy-start(bf16[2,256,2880]{1,2,0:T(8,128)(2,1)} %param.9) | copy-start | bytes 8847364
  139.9 6.1 %copy-start.11 = (bf16[1024,2880]{0,1:T(8,128)(2,1)}, bf16[1024,2880]{0,1:T(8,128)(2,1)S(1)}, u32[]{:S(2)}) copy-start(bf16[1024,2880]{0,1:T(8,128)(2,1)S(1)} %get-tuple-element.64) | copy-start | bytes 17694724
  139.9 4.3 %slice-start = ((s8[5898240]{0:T(1024)(128)(4,1)}), s8[4194304]{0:T(1024)(128)(4,1)S(1)}, s32[]{:S(2)}) async-start(s8[5898240]{0:T(1024)(128)(4,1)} %bitcast.97), calls=%async_computation.4 | async-start | bytes 8388608
  139.9 4.8 %slice-start.1 = ((s8[5898240]{0:T(1024)(128)(4,1)}), s8[1703936]{0:T(1024)(128)(4,1)S(1)}, s32[]{:S(2)}) async-start(s8[5898240]{0:T(1024)(128)(4,1)} %bitcast.97), calls=%async_computation.5 | async-start | bytes 3407872
  149.0 76.0 %all-gather.5.cloned.1.call-start = ((), (), s32[]{:S(2)}) async-start(), calls=%async_computation.2 | async-start | bytes 1548288 | tf_op jit(solution)/shard_map/all_gather | solution.py:83
  182.0 24.4 %slice-start.4 = ((s8[5898240]{0:T(1024)(128)(4,1)}), s8[1703936]{0:T(1024)(128)(4,1)S(1)}, s32[]{:S(2)}) async-start(s8[5898240]{0:T(1024)(128)(4,1)} %bitcast.102), calls=%async_computation.8 | async-start | bytes 3407872
  201.9 4.6 %slice-start.5 = ((s8[5898240]{0:T(1024)(128)(4,1)}), s8[4194304]{0:T(1024)(128)(4,1)S(1)}, s32[]{:S(2)}) async-start(s8[5898240]{0:T(1024)(128)(4,1)} %bitcast.102), calls=%async_computation.9 | async-start | bytes 8388608
Sparse Core Ops, SparseCore 0:
  33.7 48.5 all-gather.2
  149.1 31.8 reduce-scatter.3
  202.0 22.9 all-gather.4
where the time goes:
time: 238 us; the launch traced here: 237 us
  waiting for transfers between devices  93.7 us (39%)
  matrix products  58.4 us (25%)
  other arithmetic  42.2 us (18%)
  blocking collectives  19.8 us (8%)
  between operations  14.8 us (6%)
  local copies, waits for them, and re-layouts  7.99 us (3%)
    all_gather x1, waiting for transfers between devices, on_device(): lax.all_gather(predicted_maps, 'member', axis=0, tiled=True)  46.7 us
    unnamed x4, waiting for transfers between devices  32 us
    add x8, other arithmetic, lone_realization(): return (total + slope(values - other.astype(jnp.float32)[None]), None)  22.9 us
    dot_general x2, matrix products, on_device(): jnp.dot(w_out.T, prediction_adjoint, preferred_element_type=jnp.float32)  22.2 us
    dot_general x2, matrix products, on_device(): jnp.dot(w_in, hidden_codes[ensemble_position], preferred_element_type=jnp...  20 us
    psum x1, blocking collectives, on_device(): shares = lax.psum(shares, 'member')  19.8 us
    all_gather x1, waiting for transfers between devices, on_device(): summed = lax.all_gather(shares, 'space', axis=0, tiled=True)  14.9 us
    sub x8, other arithmetic, lone_realization(): return (total + slope(values - other.astype(jnp.float32)[None]), None)  8.5 us
  transfers between devices with their start and end apart: 3, of which 3 were waited for; matrix products, arithmetic and copies ran while one was open for 4% of the time, Pallas kernels for 0%

commit v1 on v0

v1 whole, which is shorter than its diff:
```python
import functools
import math

import jax
import jax.numpy as jnp
from jax import lax
from jax.experimental import pallas as pl
from jax.experimental.pallas import tpu as pltpu
from jax.sharding import PartitionSpec as P

LON = 1440
HB = 256
MESH = pl.DeviceIdType.MESH
NT = (((1,), (1,)), ((), ()))
F32 = jnp.float32
BF16 = jnp.bfloat16
K0 = math.sqrt(2.0 / math.pi)
K1 = K0 * 0.044715


def slope(diff):
    return diff * lax.rsqrt(diff * diff + 0.0625)


def kernel(
    msize,
    ssize,
    cells,
    hid_ref,
    w_in_ref,
    w_in_t_ref,
    b_in_ref,
    w_out_ref,
    w_out_t_ref,
    b_out_ref,
    tgt_ref,
    area_ref,
    code_ref,
    gwi_ref,
    gwo_ref,
    gb_ref,
    hid,
    tgt,
    act,
    dgelu,
    fcs,
    fcr,
    dfs,
    dfr,
    acc_i,
    acc_o,
    acc_b,
    half,
    r1,
    s2,
    r2,
    r3,
    full,
    x1s,
    x1r,
    x2s,
    x2r,
    p1,
    p2s,
    p2r,
    p3s,
    p3r,
    p4s,
    p4r,
    p5s,
    p5r,
):
    local = hid_ref.shape[0]
    hidden = w_in_ref.shape[0]
    latent = w_in_ref.shape[1]
    chans = w_out_ref.shape[0]
    width = hid.shape[3]
    blocks = hidden // HB
    members = local * msize
    zsize = ssize // 2
    me = lax.axis_index("member")
    sp = lax.axis_index("space")
    core = lax.rem(sp, 2)
    z = sp // 2
    partner = z * 2 + (1 - core)

    def mpeer(k):
        return lax.rem(me + k, msize)

    def zpeer(k):
        return lax.rem(z + k, zsize) * 2 + core

    barrier = pltpu.get_barrier_semaphore()
    pl.semaphore_signal(barrier, inc=1, device_id=(me, partner), device_id_type=MESH)
    for k in range(1, msize):
        pl.semaphore_signal(barrier, inc=1, device_id=(mpeer(k), sp), device_id_type=MESH)
    for k in range(1, zsize):
        pl.semaphore_signal(barrier, inc=1, device_id=(me, zpeer(k)), device_id_type=MESH)

    for c in range(msize):
        lo = c * width
        n = min(width, cells - lo)
        if n < width:
            hid[c] = jnp.zeros(hid.shape[1:], BF16)
            tgt[c] = jnp.zeros(tgt.shape[1:], BF16)
        for m in range(local):
            hid[c, m, :, :n] = hid_ref[m, :, lo : lo + n]
        tgt[c, :, :n] = tgt_ref[:, lo : lo + n]
    acc_i[...] = jnp.zeros_like(acc_i)
    acc_o[...] = jnp.zeros_like(acc_o)
    acc_b[...] = jnp.zeros_like(acc_b)

    def x1(k):
        return pltpu.make_async_remote_copy(
            src_ref=fcs.at[mpeer(k)],
            dst_ref=fcr.at[me],
            send_sem=x1s.at[k],
            recv_sem=x1r.at[k],
            device_id=(mpeer(k), sp),
            device_id_type=MESH,
        )

    def x2(k):
        return pltpu.make_async_remote_copy(
            src_ref=dfs.at[mpeer(k)],
            dst_ref=dfr.at[me],
            send_sem=x2s.at[k],
            recv_sem=x2r.at[k],
            device_id=(mpeer(k), sp),
            device_id_type=MESH,
        )

    def forward(c):
        for m in range(local):

            def block(h, carry):
                rows = pl.ds(pl.multiple_of(h * HB, HB), HB)
                x = jnp.dot(w_in_ref[rows, :], hid[c, m], preferred_element_type=F32)
                x = x + b_in_ref[rows, :]
                u = x * x
                t = jnp.tanh(x * (K0 + K1 * u))
                hx = 0.5 * x
                act[c, m, rows, :] = (hx + hx * t).astype(BF16)
                dgelu[c, m, rows, :] = (0.5 + 0.5 * t) + (hx * (1.0 - t * t)) * (
                    K0 + (3.0 * K1) * u
                )
                return carry

            lax.fori_loop(0, blocks, block, 0)
            fc = jnp.dot(w_out_ref[...], act[c, m], preferred_element_type=F32)
            fcs[c, m] = (fc + b_out_ref[...]).astype(BF16)

    def step(k, carry):
        forward(mpeer(k))

        @pl.when(k == 1)
        def _():
            pl.semaphore_wait(barrier, msize + zsize - 1)

        x1(k).start()
        return carry

    lax.fori_loop(1, msize, step, 0)
    forward(me)
    fcr[me] = fcs[me]
    for k in range(1, msize):
        x1(k).wait()

    def pairs(i, carry):
        lanes = pl.ds(pl.multiple_of(i * 128, 128), 128)
        vals = [fcr[q // local, q % local, :, lanes].astype(F32) for q in range(members)]
        total = [jnp.zeros_like(vals[0]) for q in range(members)]
        for a in range(members):
            for b in range(a + 1, members):
                s = slope(vals[a] - vals[b])
                total[a] = total[a] + s
                total[b] = total[b] - s
        goal = tgt[me, :, lanes].astype(F32)
        weight = area_ref[me, :, lanes]
        for q in range(members):
            d = weight * (slope(vals[q] - goal) - total[q] * (1.0 / members))
            dfs[q // local, q % local, :, lanes] = d.astype(BF16)
        return carry

    lax.fori_loop(0, width // 128, pairs, 0)
    for k in range(1, msize):
        x2(k).start()
    dfr[me] = dfs[me]

    def backward(c):
        for m in range(local):
            df = dfr[c, m]

            def block(h, carry):
                rows = pl.ds(pl.multiple_of(h * HB, HB), HB)
                acc_o[rows, :chans] += lax.dot_general(
                    act[c, m, rows, :], df, NT, preferred_element_type=F32
                )
                da = jnp.dot(w_out_t_ref[rows, :], df, preferred_element_type=F32)
                dp = (da * dgelu[c, m, rows, :]).astype(BF16)
                act[c, m, rows, :] = dp
                acc_i[rows, :] += lax.dot_general(
                    dp, hid[c, m], NT, preferred_element_type=F32
                )
                dpf = dp.astype(F32)
                tot = dpf[:, :128]
                for i in range(1, width // 128):
                    tot = tot + dpf[:, i * 128 : (i + 1) * 128]
                acc_b[rows, :] += tot
                return carry

            lax.fori_loop(0, blocks, block, 0)

    backward(me)

    def bstep(k, carry):
        x2(k).wait()
        backward(lax.rem(me + msize - k, msize))
        return carry

    lax.fori_loop(1, msize, bstep, 0)

    todo = [(c, m) for c in range(msize) for m in range(local)]

    def back_to_codes(count):
        for _ in range(min(count, len(todo))):
            c, m = todo.pop(0)
            lo = c * width
            n = min(width, cells - lo)
            d = jnp.dot(w_in_t_ref[...], act[c, m], preferred_element_type=F32)
            code_ref[m, :, lo : lo + n] = d[:, :n].astype(BF16)

    nrows = hidden // 2
    piece = nrows // msize

    def collect(start):
        rows = pl.ds(pl.multiple_of(start, nrows), nrows)
        bias = jnp.sum(acc_b[rows, :], axis=1, keepdims=True)
        lane = lax.broadcasted_iota(jnp.int32, (nrows, 128), 1)
        right = jnp.where(lane == chans, bias, 0.0)
        return rows, right

    def right_of(start):
        rows, bias = collect(start)
        return acc_i[rows, :], acc_o[rows, :] + bias

    li, lr = right_of((1 - core) * nrows)
    half[:, :latent] = li.astype(BF16)
    half[:, latent:] = lr.astype(BF16)
    c1 = pltpu.make_async_remote_copy(
        src_ref=half,
        dst_ref=r1,
        send_sem=p1.at[0],
        recv_sem=p1.at[1],
        device_id=(me, partner),
        device_id_type=MESH,
    )
    c1.start()
    back_to_codes(1)
    c1.wait()
    mi, mr = right_of(core * nrows)
    s2[:, :, :latent] = (mi + r1[:, :latent].astype(F32)).astype(BF16).reshape(
        msize, piece, latent
    )
    s2[:, :, latent:] = (mr + r1[:, latent:].astype(F32)).astype(BF16).reshape(
        msize, piece, 128
    )
    moves = []
    for k in range(1, msize):
        moves.append(
            pltpu.make_async_remote_copy(
                src_ref=s2.at[mpeer(k)],
                dst_ref=r2.at[k],
                send_sem=p2s.at[k],
                recv_sem=p2r.at[k],
                device_id=(mpeer(k), sp),
                device_id_type=MESH,
            )
        )
        moves[-1].start()
    back_to_codes(len(todo) // 2)
    for copy in moves:
        copy.wait()
    summed = s2[me].astype(F32)
    for k in range(1, msize):
        summed = summed + r2[k].astype(F32)
    r3[z] = summed.astype(BF16)
    moves = []
    for k in range(1, zsize):
        moves.append(
            pltpu.make_async_remote_copy(
                src_ref=r3.at[z],
                dst_ref=r3.at[z],
                send_sem=p3s.at[k],
                recv_sem=p3r.at[k],
                device_id=(me, zpeer(k)),
                device_id_type=MESH,
            )
        )
        moves[-1].start()
    back_to_codes(len(todo))
    for copy in moves:
        copy.wait()
    summed = r3[0].astype(F32)
    for k in range(1, zsize):
        summed = summed + r3[k].astype(F32)
    full[core, me] = summed.astype(BF16)

    def share(k):
        return pltpu.make_async_remote_copy(
            src_ref=full.at[core, me],
            dst_ref=full.at[core, me],
            send_sem=p4s.at[k],
            recv_sem=p4r.at[k],
            device_id=(mpeer(k), sp),
            device_id_type=MESH,
        )

    def across(k):
        owner = lax.rem(me + msize - k, msize)
        return pltpu.make_async_remote_copy(
            src_ref=full.at[core, owner],
            dst_ref=full.at[core, owner],
            send_sem=p5s.at[k],
            recv_sem=p5r.at[k],
            device_id=(me, partner),
            device_id_type=MESH,
        )

    for k in range(1, msize):
        share(k).start()
    across(0).start()
    for k in range(1, msize):
        share(k).wait()
        across(k).start()
    for k in range(msize):
        across(k).wait()
    scale = 1.0 / math.sqrt(members * cells)
    for side in range(2):
        for m in range(msize):
            lo = side * nrows + m * piece
            gwi_ref[lo : lo + piece, :] = full[side, m, :, :latent].astype(F32) * scale
            acc_o[lo : lo + piece, :] = full[side, m, :, latent:].astype(F32) * scale
    turned = jnp.transpose(acc_o[...])
    gwo_ref[...] = turned[:chans]
    gb_ref[...] = turned[chans : chans + 1]


def on_device(hidden_codes, w_in, b_in, w_out, b_out, target, band_start):
    local, latent, cells = hidden_codes.shape
    hidden = w_in.shape[0]
    chans = w_out.shape[0]
    msize = lax.axis_size("member")
    ssize = lax.axis_size("space")
    zsize = ssize // 2
    rows = cells // LON
    lat_rows = rows * ssize
    tiles = -(-cells // 128)
    width = -(-tiles // msize) * 128
    place = jnp.arange(msize * width, dtype=jnp.int32)
    angle = ((band_start[0] + place // LON).astype(F32) + 0.5) * (
        math.pi / lat_rows
    ) - math.pi / 2
    area = jnp.where(place < cells, jnp.cos(angle), 0.0).reshape(msize, 1, width)
    nrows = hidden // 2
    piece = nrows // msize
    wide = latent + 128
    vmem = pl.BlockSpec(memory_space=pltpu.VMEM)
    dma = pltpu.SemaphoreType.DMA
    code, gwi, gwo, gb = pl.pallas_call(
        functools.partial(kernel, msize, ssize, cells),
        out_shape=(
            jax.ShapeDtypeStruct((local, latent, cells), BF16),
            jax.ShapeDtypeStruct((hidden, latent), F32),
            jax.ShapeDtypeStruct((chans, hidden), F32),
            jax.ShapeDtypeStruct((1, hidden), F32),
        ),
        in_specs=[vmem] * 9,
        out_specs=(vmem,) * 4,
        scratch_shapes=[
            pltpu.VMEM((msize, local, latent, width), BF16),
            pltpu.VMEM((msize, chans, width), BF16),
            pltpu.VMEM((msize, local, hidden, width), BF16),
            pltpu.VMEM((msize, local, hidden, width), F32),
            pltpu.VMEM((msize, local, chans, width), BF16),
            pltpu.VMEM((msize, local, chans, width), BF16),
            pltpu.VMEM((msize, local, chans, width), BF16),
            pltpu.VMEM((msize, local, chans, width), BF16),
            pltpu.VMEM((hidden, latent), F32),
            pltpu.VMEM((hidden, 128), F32),
            pltpu.VMEM((hidden, 128), F32),
            pltpu.VMEM((nrows, wide), BF16),
            pltpu.VMEM((nrows, wide), BF16),
            pltpu.VMEM((msize, piece, wide), BF16),
            pltpu.VMEM((msize, piece, wide), BF16),
            pltpu.VMEM((zsize, piece, wide), BF16),
            pltpu.VMEM((2, msize, piece, wide), BF16),
            dma((msize,)),
            dma((msize,)),
            dma((msize,)),
            dma((msize,)),
            dma((2,)),
            dma((msize,)),
            dma((msize,)),
            dma((zsize,)),
            dma((zsize,)),
            dma((msize,)),
            dma((msize,)),
            dma((msize,)),
            dma((msize,)),
        ],
        compiler_params=pltpu.CompilerParams(
            collective_id=0, has_side_effects=True, vmem_limit_bytes=67043328
        ),
    )(
        hidden_codes,
        w_in,
        w_in.T,
        b_in[:, None],
        w_out,
        w_out.T,
        b_out[:, None],
        target,
        area,
    )
    return code, gwi, gwo, gb[0]


def solution(mesh):
    in_specs = (P("member", None, "space"), P(), P(), P(), P(), P(None, "space"), P("space"))
    out_specs = (P("member", None, "space"), P(), P(), P())
    return jax.shard_map(
        on_device, mesh=mesh, in_specs=in_specs, out_specs=out_specs, check_vma=False
    )
```

time: 238 us -> 104 us (0.44)
  waiting for transfers between devices: 93.7 us -> 0 us
  Pallas kernels: 0 us -> 82.6 us
  matrix products: 58.4 us -> 0 us
  other arithmetic: 42.2 us -> 0.95 us
  blocking collectives: 19.8 us -> 0 us
  between operations: 14.8 us -> 1.31 us
  local copies, waits for them, and re-layouts: 7.99 us -> 18.4 us
    pallas_call x0 -> x1, Pallas kernels: none -> 82.6 us  [on_device(): pl.pallas_call(functools.partial(kernel, msize, ssize, cells), out_shape=...]
    all_gather x2 -> x0, waiting for transfers between devices: 61.6 us -> none  [the longest x1 46.7 us: on_device(): lax.all_gather(predicted_maps, 'member', axis=0, tiled=True)]
    dot_general x12 -> x0, matrix products: 58.4 us -> none  [the longest x2 22.2 us: on_device(): jnp.dot(w_out.T, prediction_adjoint, preferred_element_type=jnp.float32)]
    unnamed x4 -> x0, waiting for transfers between devices: 32 us -> none
    add x8 -> x0, other arithmetic: 22.9 us -> none  [lone_realization(): return (total + slope(values - other.astype(jnp.float32)[None]), None)]
    psum x1 -> x0, blocking collectives: 19.8 us -> none  [on_device(): shares = lax.psum(shares, 'member')]
    sub x8 -> x0, other arithmetic: 8.5 us -> none  [lone_realization(): return (total + slope(values - other.astype(jnp.float32)[None]), None)]
    unnamed x47 -> x13, local copies, waits for them, and re-layouts: 7.83 us -> 15.3 us
  transfers between devices with their start and end apart: 3 -> 0, of which waited for: 3 -> 0; matrix products, arithmetic and copies ran while one was open for 4% -> 0% of each run, Pallas kernels for 0% -> 0%
where the time goes in v1:
time: 104 us; the launch traced here: 103 us
  Pallas kernels  82.6 us (79%)
  local copies, waits for them, and re-layouts  18.4 us (18%)
  between operations  1.31 us (1%)
    pallas_call x1, Pallas kernels, on_device(): pl.pallas_call(functools.partial(kernel, msize, ssize, cells), out_shape=...  82.6 us
    unnamed x13, local copies, waits for them, and re-layouts  15.3 us

profile of v1, /device:TPU:0, one launch (start us, length us, event | category | flops | bytes accessed | tf_op | source)
XLA Modules:
  0.0 103.3 jit_solution(9855135605525509530)
XLA Ops:
  1.3 1.0 compare_select_fusion.area_ref
  2.2 1.4 %copy.20.b_out_ref = f32[72,1]{1,0:T(8,128)} copy(f32[72,1]{0,1:T(1,128)} %bitcast.11) | data formatting | bytes 576 | tf_op jit(solution)/shard_map/broadcast_in_dim | solution.py:422
  3.6 1.7 %copy.17 = bf16[72,1024]{0,1:T(8,128)(2,1)} copy(bf16[72,1024]{1,0:T(8,128)(2,1)} %w_out_ref.1) | data formatting | bytes 294912 | tf_op args[3]
  5.3 1.7 %copy.19.b_in_ref = f32[1024,1]{1,0:T(8,128)} copy(f32[1024,1]{0,1:T(1,128)} %bitcast.9) | data formatting | bytes 8192 | tf_op jit(solution)/shard_map/broadcast_in_dim | solution.py:419
  7.0 2.0 %copy.16 = bf16[1024,256]{0,1:T(8,128)(2,1)} copy(bf16[1024,256]{1,0:T(8,128)(2,1)} %w_in_ref.1) | data formatting | bytes 1048576 | tf_op args[1]
  9.1 4.6 %copy.18.hid_ref = bf16[2,256,2880]{2,1,0:T(8,128)(2,1)} copy(bf16[2,256,2880]{1,2,0:T(8,128)(2,1)} %param.7) | data formatting | bytes 5898240 | tf_op args[0]
  13.7 82.6 %shard_map.102 = (bf16[2,256,2880]{2,1,0:T(8,128)(2,1)}, f32[1024,256]{1,0:T(8,128)}, f32[72,1024]{1,0:T(8,128)}, f32[1,1024]{1,0:T(1,128)}) custom-call(bf16[2,256,2880]{2,1,0:T(8,128)(2,1)} %copy.18.hid_ref, bf16[1024,256]{1,0:T(8,128)(2,1)} %w_in_ref.1, bf16[256,1024]{1,0:T(8,128)(2,1)} %bitcast.7, f32[1024,1]{1,0:T(8,128)} %copy.19.b_in_ref, ...), custom_call_target="tpu_custom_call" | custom-call | tf_op jit(solution)/shard_map/pallas_call | solution.py:370
  96.3 0.0 copy-start
  96.3 0.0 copy-start.1
  96.3 0.0 copy-start.2
  96.3 4.7 %copy.21 = bf16[2,256,2880]{1,2,0:T(8,128)(2,1)} copy(bf16[2,256,2880]{2,1,0:T(8,128)(2,1)} %get-tuple-element.16) | data formatting | bytes 5898240
  101.0 0.0 copy-done
  101.0 1.0 copy.26
  102.0 0.0 copy-done.1
  102.0 0.7 copy.27
  102.7 0.0 copy-done.2
  102.7 0.6 copy.28
Async XLA Ops:
  96.3 4.7 %copy-start = (f32[1024,256]{1,0:T(8,128)S(1)}, f32[1024,256]{1,0:T(8,128)}, u32[]{:S(2)}) copy-start(f32[1024,256]{1,0:T(8,128)} %get-tuple-element.25) | copy-start | bytes 3145732
  96.3 5.7 %copy-start.1 = (f32[72,1024]{1,0:T(8,128)S(1)}, f32[72,1024]{1,0:T(8,128)}, u32[]{:S(2)}) copy-start(f32[72,1024]{1,0:T(8,128)} %get-tuple-element.26) | copy-start | bytes 884740
  96.3 6.4 %copy-start.2 = (f32[1,1024]{1,0:T(1,128)S(1)}, f32[1,1024]{1,0:T(1,128)}, u32[]{:S(2)}) copy-start(f32[1,1024]{1,0:T(1,128)} %get-tuple-element.11) | copy-start | bytes 12292

commit v2 on v1

--- a/solution.py
+++ b/solution.py
@@ -28,10 +28,8 @@
     cells,
     hid_ref,
     w_in_ref,
-    w_in_t_ref,
     b_in_ref,
     w_out_ref,
-    w_out_t_ref,
     b_out_ref,
     tgt_ref,
     area_ref,
@@ -69,12 +67,18 @@
     p4r,
     p5s,
     p5r,
+    w_in_t,
+    w_out_t,
+    b_in,
+    b_out,
+    load,
+    save,
 ):
     local = hid_ref.shape[0]
     hidden = w_in_ref.shape[0]
     latent = w_in_ref.shape[1]
     chans = w_out_ref.shape[0]
-    width = hid.shape[3]
+    width = hid.shape[2]
     blocks = hidden // HB
     members = local * msize
     zsize = ssize // 2
@@ -97,15 +101,34 @@
     for k in range(1, zsize):
         pl.semaphore_signal(barrier, inc=1, device_id=(me, zpeer(k)), device_id_type=MESH)
 
+    last = msize - 1
+    rest = cells - last * width
+
+    def span(c):
+        return width if c < last else rest
+
+    def fetch(c, m, n, lo):
+        return pltpu.make_async_copy(
+            hid_ref.at[m, pl.ds(lo, n)], hid.at[c, m, pl.ds(0, n)], load.at[c, m]
+        )
+
+    def put(c, m):
+        n = span(c)
+        return pltpu.make_async_copy(
+            hid.at[c, m, pl.ds(0, n)], code_ref.at[m, pl.ds(c * width, n)], save.at[c, m]
+        )
+
     for c in range(msize):
-        lo = c * width
-        n = min(width, cells - lo)
-        if n < width:
-            hid[c] = jnp.zeros(hid.shape[1:], BF16)
-            tgt[c] = jnp.zeros(tgt.shape[1:], BF16)
         for m in range(local):
-            hid[c, m, :, :n] = hid_ref[m, :, lo : lo + n]
-        tgt[c, :, :n] = tgt_ref[:, lo : lo + n]
+            fetch(c, m, span(c), c * width).start()
+    if rest < width:
+        hid[last, :, rest:, :] = jnp.zeros((local, width - rest, latent), BF16)
+        tgt[last] = jnp.zeros(tgt.shape[1:], BF16)
+    for c in range(msize):
+        n = span(c)
+        tgt[c, :, :n] = tgt_ref[:, c * width : c * width + n]
+    b_in[...] = jnp.transpose(jnp.broadcast_to(b_in_ref[...], (128, hidden)))
+    b_out[...] = jnp.transpose(jnp.broadcast_to(b_out_ref[...], (128, chans)))
     acc_i[...] = jnp.zeros_like(acc_i)
     acc_o[...] = jnp.zeros_like(acc_o)
     acc_b[...] = jnp.zeros_like(acc_b)
@@ -133,22 +156,30 @@
     def forward(c):
         for m in range(local):
 
+            @pl.when(c < last)
+            def _():
+                fetch(c, m, width, 0).wait()
+
+            @pl.when(c == last)
+            def _():
+                fetch(c, m, rest, 0).wait()
+
             def block(h, carry):
                 rows = pl.ds(pl.multiple_of(h * HB, HB), HB)
-                x = jnp.dot(w_in_ref[rows, :], hid[c, m], preferred_element_type=F32)
-                x = x + b_in_ref[rows, :]
+                x = lax.dot_general(
+                    w_in_ref[rows, :], hid[c, m], NT, preferred_element_type=F32
+                )
+                x = x + b_in[rows, :1]
                 u = x * x
-                t = jnp.tanh(x * (K0 + K1 * u))
-                hx = 0.5 * x
-                act[c, m, rows, :] = (hx + hx * t).astype(BF16)
-                dgelu[c, m, rows, :] = (0.5 + 0.5 * t) + (hx * (1.0 - t * t)) * (
-                    K0 + (3.0 * K1) * u
-                )
+                s = 0.5 + 0.5 * jnp.tanh(x * (K0 + K1 * u))
+                g = x * s
+                act[c, m, rows, :] = g.astype(BF16)
+                dgelu[c, m, rows, :] = s + (g * (1.0 - s)) * (2.0 * K0 + (6.0 * K1) * u)
                 return carry
 
             lax.fori_loop(0, blocks, block, 0)
             fc = jnp.dot(w_out_ref[...], act[c, m], preferred_element_type=F32)
-            fcs[c, m] = (fc + b_out_ref[...]).astype(BF16)
+            fcs[c, m] = (fc + b_out[:, :1]).astype(BF16)
 
     def step(k, carry):
         forward(mpeer(k))
@@ -163,6 +194,8 @@
     lax.fori_loop(1, msize, step, 0)
     forward(me)
     fcr[me] = fcs[me]
+    w_in_t[...] = jnp.transpose(w_in_ref[...])
+    w_out_t[...] = jnp.transpose(w_out_ref[...].astype(F32)).astype(BF16)
     for k in range(1, msize):
         x1(k).wait()
 
@@ -196,12 +229,10 @@
                 acc_o[rows, :chans] += lax.dot_general(
                     act[c, m, rows, :], df, NT, preferred_element_type=F32
                 )
-                da = jnp.dot(w_out_t_ref[rows, :], df, preferred_element_type=F32)
+                da = jnp.dot(w_out_t[rows, :], df, preferred_element_type=F32)
                 dp = (da * dgelu[c, m, rows, :]).astype(BF16)
                 act[c, m, rows, :] = dp
-                acc_i[rows, :] += lax.dot_general(
-                    dp, hid[c, m], NT, preferred_element_type=F32
-                )
+                acc_i[rows, :] += jnp.dot(dp, hid[c, m], preferred_element_type=F32)
                 dpf = dp.astype(F32)
                 tot = dpf[:, :128]
                 for i in range(1, width // 128):
@@ -225,10 +256,9 @@
     def back_to_codes(count):
         for _ in range(min(count, len(todo))):
             c, m = todo.pop(0)
-            lo = c * width
-            n = min(width, cells - lo)
-            d = jnp.dot(w_in_t_ref[...], act[c, m], preferred_element_type=F32)
-            code_ref[m, :, lo : lo + n] = d[:, :n].astype(BF16)
+            d = jnp.dot(w_in_t[...], act[c, m], preferred_element_type=F32)
+            hid[c, m] = jnp.transpose(d.astype(BF16))
+            put(c, m).start()
 
     nrows = hidden // 2
     piece = nrows // msize
@@ -344,6 +374,9 @@
     turned = jnp.transpose(acc_o[...])
     gwo_ref[...] = turned[:chans]
     gb_ref[...] = turned[chans : chans + 1]
+    for c in range(msize):
+        for m in range(local):
+            put(c, m).wait()
 
 
 def on_device(hidden_codes, w_in, b_in, w_out, b_out, target, band_start):
@@ -370,15 +403,15 @@
     code, gwi, gwo, gb = pl.pallas_call(
         functools.partial(kernel, msize, ssize, cells),
         out_shape=(
-            jax.ShapeDtypeStruct((local, latent, cells), BF16),
+            jax.ShapeDtypeStruct((local, cells, latent), BF16),
             jax.ShapeDtypeStruct((hidden, latent), F32),
             jax.ShapeDtypeStruct((chans, hidden), F32),
             jax.ShapeDtypeStruct((1, hidden), F32),
         ),
-        in_specs=[vmem] * 9,
-        out_specs=(vmem,) * 4,
+        in_specs=[pl.BlockSpec(memory_space=pl.ANY)] + [vmem] * 6,
+        out_specs=(pl.BlockSpec(memory_space=pl.ANY),) + (vmem,) * 3,
         scratch_shapes=[
-            pltpu.VMEM((msize, local, latent, width), BF16),
+            pltpu.VMEM((msize, local, width, latent), BF16),
             pltpu.VMEM((msize, chans, width), BF16),
             pltpu.VMEM((msize, local, hidden, width), BF16),
             pltpu.VMEM((msize, local, hidden, width), F32),
@@ -408,22 +441,26 @@
             dma((msize,)),
             dma((msize,)),
             dma((msize,)),
+            pltpu.VMEM((latent, hidden), BF16),
+            pltpu.VMEM((hidden, chans), BF16),
+            pltpu.VMEM((hidden, 128), F32),
+            pltpu.VMEM((chans, 128), F32),
+            dma((msize, local)),
+            dma((msize, local)),
         ],
         compiler_params=pltpu.CompilerParams(
             collective_id=0, has_side_effects=True, vmem_limit_bytes=67043328
         ),
     )(
-        hidden_codes,
+        jnp.swapaxes(hidden_codes, 1, 2),
         w_in,
-        w_in.T,
-        b_in[:, None],
+        b_in[None, :],
         w_out,
-        w_out.T,
-        b_out[:, None],
+        b_out[None, :],
         target,
         area,
     )
-    return code, gwi, gwo, gb[0]
+    return jnp.swapaxes(code, 1, 2), gwi, gwo, gb[0]
 
 
 def solution(mesh):

time: 104 us -> 89 us (0.86)
  local copies, waits for them, and re-layouts: 18.4 us -> 6.01 us
  Pallas kernels: 82.6 us -> 80.6 us
    unnamed x13 -> x10, local copies, waits for them, and re-layouts: 15.3 us -> 6.01 us
    broadcast_in_dim x2 -> x0, local copies, waits for them, and re-layouts: 3.06 us -> none  [the longest x1 1.71 us: on_device(): b_in[:, None]]
    pallas_call x1, Pallas kernels: 82.6 us -> 80.6 us  [on_device(): pl.pallas_call(functools.partial(kernel, msize, ssize, cells), out_shape=...]
where the time goes in v2:
time: 89 us; the launch traced here: 88.8 us
  Pallas kernels  80.6 us (91%)
  local copies, waits for them, and re-layouts  6.01 us (7%)
  between operations  1.31 us (1%)
  other arithmetic  0.96 us (1%)
    pallas_call x1, Pallas kernels, on_device(): pl.pallas_call(functools.partial(kernel, msize, ssize, cells), out_shape=...  80.6 us
    unnamed x10, local copies, waits for them, and re-layouts  6.01 us

profile of v2, /device:TPU:0, one launch (start us, length us, event | category | flops | bytes accessed | tf_op | source)
XLA Modules:
  0.0 88.8 jit_solution(12433758501792038973)
XLA Ops:
  1.3 1.0 %compare_select_fusion.area_ref = f32[4,1,768]{2,1,0:T(1,128)} fusion(s32[]{:T(128)} %bitcast.6), kind=kLoop, calls=%fused_computation.1 | loop fusion | flops 52224 | bytes 12292 | tf_op jit(solution)/shard_map/jit(_where)/select_n | solution.py:397
  2.2 80.6 %shard_map.102 = (bf16[2,2880,256]{2,1,0:T(8,128)(2,1)}, f32[1024,256]{1,0:T(8,128)}, f32[72,1024]{1,0:T(8,128)}, f32[1,1024]{1,0:T(1,128)}) custom-call(bf16[2,2880,256]{2,1,0:T(8,128)(2,1)} %bitcast.7, bf16[1024,256]{1,0:T(8,128)(2,1)} %w_in_ref.1, f32[1,1024]{1,0:T(1,128)} %bitcast.9, bf16[72,1024]{1,0:T(8,128)(2,1)} %w_out_ref.1, f32[1,72]{1,0:T(1,128)} %bitcast.11, ...), custom_call_target="tpu_custom_call" | custom-call | tf_op jit(solution)/shard_map/pallas_call | solution.py:403
  82.8 0.0 copy-start
  82.8 0.0 copy-start.1
  82.8 0.0 copy-start.2
  82.8 3.7 %copy.16 = bf16[2,256,2880]{1,2,0:T(8,128)(2,1)} copy(bf16[2,256,2880]{1,2,0:T(8,128)(2,1)} %bitcast.8) | data formatting | bytes 5898240
  86.5 0.0 copy-done
  86.6 1.0 %copy.17 = f32[1024,256]{1,0:T(8,128)} copy(f32[1024,256]{1,0:T(8,128)S(1)} %copy-done) | data formatting | bytes 2097152
  87.5 0.0 copy-done.1
  87.5 0.7 copy.18
  88.2 0.0 copy-done.2
  88.2 0.6 copy.19
Async XLA Ops:
  82.8 3.8 %copy-start = (f32[1024,256]{1,0:T(8,128)S(1)}, f32[1024,256]{1,0:T(8,128)}, u32[]{:S(2)}) copy-start(f32[1024,256]{1,0:T(8,128)} %get-tuple-element.17) | copy-start | bytes 3145732
  82.8 4.7 %copy-start.1 = (f32[72,1024]{1,0:T(8,128)S(1)}, f32[72,1024]{1,0:T(8,128)}, u32[]{:S(2)}) copy-start(f32[72,1024]{1,0:T(8,128)} %get-tuple-element.18) | copy-start | bytes 884740
  82.8 5.4 %copy-start.2 = (f32[1,1024]{1,0:T(1,128)S(1)}, f32[1,1024]{1,0:T(1,128)}, u32[]{:S(2)}) copy-start(f32[1,1024]{1,0:T(1,128)} %get-tuple-element.11) | copy-start | bytes 12292
